TPU v7x, 32 devices: a whole 2x2x4 slice. The times are simulated.
32 devices in a mesh: grp: 8 (over y, x, core), inner: 4 (over z).
Axes of the slice: x: 2, y: 2, z: 4, core: 2. Of those that a mesh axis runs over, the one named last changes fastest.
Arguments:
- amplitudes: bfloat16 [16, 8, 12288], P('grp', None, 'inner'), may hold values from -6 to 6
- factors: bfloat16 [16, 2000, 12288], P('grp', 'inner'), may hold values from -0.125 to 0.125
- atom_charges: bfloat16 [16, 64, 12288], P('grp', None, 'inner'), may hold values from -0.0068359375 to 0.0068359375
- eps_occ: float32 [16, 48], P('grp'), may hold values from -1.2 to -0.3
- eps_vir: float32 [16, 256], P('grp'), may hold values from 0.1 to 1.5
- occ_count: int32 [16], P('grp'), may hold values from 24 to 48
- vir_count: int32 [16], P('grp'), may hold values from 128 to 256
- atom_list: int32 [1024], P('grp'), may hold values from 0 to 1023, each once
- positions: float32 [3, 1024], replicated, may hold values from 0 to 12
Outputs:
- refined: float32 [16, 8, 12288], P('grp', None, 'inner')
- hamiltonian: float32 [128, 8, 16], P('grp', None, 'inner')
Inputs may be any that keep to these rules, and one draw needn't show every extreme that they name: `atom_list`: every atom index appears exactly once.
All inputs are finite; a program needn't handle non-finite values.
Results may differ from a plain program's by a relative error of at most 0.022.
Values may be sent and summed in bfloat16 or wider, within the bound.
No kernel may reach another device: no remote copies, remote signals or barrier semaphores. Data moves between devices by JAX's collectives and lax.ppermute only.
A program may use at most 64 MiB of HBM per device.

v0:
```python
import jax
import jax.numpy as jnp
from jax import lax
from jax.sharding import PartitionSpec as P

NVIR = 256
STATES = 8
epsilon = 1e-06


def coupling_block(
    group_charges, own_xyz, own_ids, energies, in_charges, in_xyz, slice_rows, inner_pos, monomers
):
    count = in_charges.shape[0]
    offset = own_xyz[:, :, :, None, None] - jnp.transpose(in_xyz, (1, 0, 2))[None, :, None, :, :]
    kernel = 1.0 / jnp.sqrt(jnp.sum(offset * offset, axis=1) + 1.0)
    block = jnp.einsum(
        "csa,carb,rb->csr", group_charges, kernel, in_charges, precision=lax.Precision.HIGHEST
    )
    column = jnp.arange(count, dtype=jnp.int32)
    source = column // slice_rows
    within = inner_pos * slice_rows + column % slice_rows
    in_ids = source * monomers + within // STATES
    in_state = within % STATES
    same = own_ids[:, None, None] == in_ids[None, None, :]
    diag = jnp.arange(STATES, dtype=jnp.int32)[None, :, None] == in_state[None, None, :]
    block = jnp.where(same, jnp.where(diag, energies[:, :, None], 0.0), block)
    return block.reshape(monomers * STATES, count)


def local(
    amplitudes, factors, atom_charges, eps_occ, eps_vir, occ_count, vir_count, atom_list, positions
):
    monomers, states_here, local_pairs = amplitudes.shape
    atom_count = atom_charges.shape[1]
    inner_count = lax.axis_size("inner")
    inner_pos = lax.axis_index("inner")
    pair_index = inner_pos * local_pairs + jnp.arange(local_pairs, dtype=jnp.int32)
    occ_of = pair_index // NVIR
    vir_of = pair_index % NVIR
    active = (
        (occ_of[None, :] < occ_count[:, None]) & (vir_of[None, :] < vir_count[:, None])
    ).astype(jnp.float32)
    gap = jnp.take(eps_vir, vir_of, axis=1) - jnp.take(eps_occ, occ_of, axis=1)
    masked = amplitudes * active[:, None, :].astype(jnp.bfloat16)
    fitted = jnp.einsum(
        "cso,cqo->csq",
        lax.all_gather(masked, "inner", axis=2, tiled=True),
        factors,
        preferred_element_type=jnp.float32,
    )
    fitted_low = fitted.astype(jnp.bfloat16)
    current = masked.astype(jnp.float32)
    partial_value = (
        2.0 * jnp.einsum("csq,cqo->cso", fitted_low, factors, preferred_element_type=jnp.float32)
    ).astype(jnp.bfloat16)
    coulomb = lax.psum_scatter(partial_value, "inner", scatter_dimension=2, tiled=True).astype(
        jnp.float32
    )
    image = gap[:, None, :] * current + coulomb * active[:, None, :]
    numerator, squares = lax.psum(
        (jnp.sum(current * image, axis=2), jnp.sum(current * current, axis=2)), "inner"
    )
    energies = numerator / (squares + epsilon)
    refined = active[:, None, :] * (
        current - (image - energies[:, :, None] * current) / gap[:, None, :]
    )
    refined_low = refined.astype(jnp.bfloat16)
    partial_charges = jnp.einsum(
        "cso,cao->csa", refined_low, atom_charges, preferred_element_type=jnp.float32
    ).reshape(monomers * states_here, atom_count)
    slice_rows = monomers * states_here // inner_count
    group_charges = lax.psum(partial_charges, "inner")
    slice_charges = lax.dynamic_slice_in_dim(group_charges, inner_pos * slice_rows, slice_rows, 0)
    group_charges = group_charges.reshape(monomers, states_here, atom_count)
    own_xyz = (
        jnp.take(positions, atom_list, axis=1).reshape(3, monomers, atom_count).transpose(1, 0, 2)
    )
    slice_index = inner_pos * slice_rows + jnp.arange(slice_rows, dtype=jnp.int32)
    slice_xyz = jnp.take(own_xyz, slice_index // STATES, axis=0)
    group_pos = lax.axis_index("grp")
    groups = lax.axis_size("grp")
    own_ids = group_pos * monomers + jnp.arange(monomers, dtype=jnp.int32)
    block = coupling_block(
        group_charges,
        own_xyz,
        own_ids,
        energies,
        lax.all_gather(slice_charges, "grp", axis=0, tiled=True),
        lax.all_gather(slice_xyz, "grp", axis=0, tiled=True),
        slice_rows,
        inner_pos,
        monomers,
    )
    return (refined, block.reshape(monomers * states_here, groups, slice_rows))


def solution(mesh):
    in_specs = (
        P("grp", None, "inner"),
        P("grp", "inner", None),
        P("grp", None, "inner"),
        P("grp", None),
        P("grp", None),
        P("grp"),
        P("grp"),
        P("grp"),
        P(),
    )
    out_specs = (P("grp", None, "inner"), P("grp", None, "inner"))
    return jax.shard_map(local, mesh=mesh, in_specs=in_specs, out_specs=out_specs, check_vma=False)
```

profile of v0, /device:TPU:0, one launch (start us, length us, event | category | flops | bytes accessed | tf_op | source)
XLA Modules:
  0.0 175.4 jit_solution(12270682259931202777)
XLA Ops:
  7.3 0.8 fusion.36
  8.1 0.9 broadcast_multiply_fusion
  9.0 16.3 %all_gather.9 = bf16[2,8,12288]{2,1,0:T(8,128)(2,1)S(1)} all-gather(bf16[2,8,3072]{2,1,0:T(8,128)(2,1)S(1)} %broadcast_multiply_fusion), channel_id=1, replica_groups=mesh['grp'=8,'inner'=4] {'inner'}, dimensions={2}, use_global_device_ids=true | all-gather | bytes 491520 | tf_op jit(solution)/shard_map/all_gather | solution.py:48
  25.3 64.8 %fusion.7 = bf16[2,8,12288]{2,1,0:T(8,128)(2,1)} fusion(bf16[2,500,12288]{2,0,1:T(2,128)(2,1)} %param.10, bf16[2,8,12288]{2,1,0:T(8,128)(2,1)S(1)} %all_gather.9), kind=kOutput, calls=%fused_computation.9 | convolution fusion | flops 393617216 | bytes 25362432 | tf_op jit(solution)/shard_map/csq,cqo->cso/dot_general | solution.py:55
  90.6 10.8 %gather_fusion = f32[3072,2]{1,0:T(8,128)} fusion(f32[2,256]{0,1:T(8,128)S(1)} %copy.45, s32[3072]{0:T(1024)S(1)} %broadcast_clamp_fusion.1), kind=kCustom, calls=%fused_computation | custom fusion | bytes 61440 | tf_op jit(solution)/shard_map/jit(_take)/gather | solution.py:44
  101.4 10.8 %gather_fusion.1 = f32[3072,2]{1,0:T(8,128)} fusion(f32[2,48]{0,1:T(8,128)S(1)} %copy.46, s32[3072]{0:T(1024)S(1)} %broadcast_clamp_fusion), kind=kCustom, calls=%fused_computation.1 | custom fusion | bytes 61440 | tf_op jit(solution)/shard_map/jit(_take)/gather | solution.py:44
  112.2 3.8 %subtract_bitcast_fusion = f32[2,3072]{0,1:T(8,128)S(1)} fusion(f32[3072,2]{1,0:T(8,128)} %gather_fusion.1, f32[3072,2]{1,0:T(8,128)} %gather_fusion, pred[3072]{0:T(1024)(128)(4,1)S(1)} %get-tuple-element.14, pred[3072]{0:T(1024)(128)(4,1)S(1)} %get-tuple-element.15), kind=kLoop, calls=%fused_computation.14 | loop fusion | flops 18432 | bytes 79872 | tf_op jit(solution)/shard_map/sub | solution.py:44
  116.0 0.5 copy.47
  116.5 0.2 copy.50
  116.7 0.6 gather_fusion.2
  117.6 0.6 gather_fusion.3
  118.2 9.2 %all_gather.10 = f32[32,3,64]{2,1,0:T(4,128)S(1)} all-gather(f32[4,3,64]{2,1,0:T(4,128)S(1)} %broadcast_select_fusion), channel_id=1, replica_groups=mesh['grp'=8,'inner'=4] {'grp'}, dimensions={0}, use_global_device_ids=true | all-gather | bytes 27648 | tf_op jit(solution)/shard_map/all_gather | solution.py:90
  127.5 1.1 multiply_reduce_fusion
  128.7 0.3 add_rsqrt_fusion
  129.0 0.6 copy-done.1
  129.6 1.1 fusion.19
  130.6 12.4 %all-reduce = (f32[2,8]{1,0:T(2,128)S(1)}, f32[2,8]{1,0:T(2,128)S(1)}) all-reduce(f32[2,8]{1,0:T(2,128)S(1)} %get-tuple-element.5, f32[2,8]{1,0:T(2,128)S(1)} %get-tuple-element.4), channel_id=1, replica_groups=mesh['grp'=8,'inner'=4] {'inner'}, use_global_device_ids=true, to_apply=%region_2.3 | all-reduce | flops 32 | bytes 256 | tf_op jit(solution)/shard_map/psum | solution.py:61
  143.1 1.0 fusion.22
  144.1 0.3 convolution_bitcast_fusion
  144.4 8.5 %psum.23 = f32[16,64]{1,0:T(8,128)S(1)} all-reduce(f32[16,64]{1,0:T(8,128)S(1)} %convolution_bitcast_fusion), channel_id=1, replica_groups=mesh['grp'=8,'inner'=4] {'inner'}, use_global_device_ids=true, to_apply=%region_5.6 | all-reduce | flops 1024 | bytes 8192 | tf_op jit(solution)/shard_map/psum | solution.py:73
  152.9 8.9 %all-gather = f32[8,4,64]{2,1,0:T(4,128)S(1)} all-gather(f32[1,4,64]{2,1,0:T(4,128)S(1)} %dynamic-slice_bitcast_fusion), channel_id=1, replica_groups=mesh['grp'=8,'inner'=4] {'grp'}, dimensions={0}, use_global_device_ids=true | all-gather | bytes 9216 | tf_op jit(solution)/shard_map/all_gather | solution.py:89
  161.8 5.8 %fusion.10 = f32[32,1,2,64]{3,1,2,0:T(1,128)S(1)} fusion(f32[32,64,1,1]{1,2,3,0:T(1,128)S(1)} %bitcast.34, f32[2,64,32,64]{3,2,1,0:T(8,128)S(1)} %add_rsqrt_fusion), kind=kOutput, calls=%fused_computation.11 | convolution fusion | flops 3145728 | bytes 1073152 | tf_op jit(solution)/shard_map/csa,carb,rb->csr/dot_general | solution.py:17
  167.6 0.2 convolution_select_fusion
  167.9 0.7 reshape_reshape.3
  (41 shorter events, 1.0 us)
Async XLA Ops:
  7.2 136.9 %copy-start = (bf16[2,64,3072]{2,1,0:T(8,128)(2,1)S(1)}, bf16[2,64,3072]{2,1,0:T(8,128)(2,1)}, u32[]{:S(2)}) copy-start(bf16[2,64,3072]{2,1,0:T(8,128)(2,1)} %param.11) | copy-start | bytes 2359300
  7.2 121.8 %reduce-scatter.2.cloned.1.call-start = ((), (), s32[]{:S(2)}) async-start(), calls=%async_computation.1 | async-start | bytes 491520 | tf_op jit(solution)/shard_map/reduce_scatter | solution.py:57
  25.3 65.0 %copy-start.6 = (s32[128]{0:T(128)S(1)}, s32[128]{0:T(128)}, u32[]{:S(2)}) copy-start(s32[128]{0:T(128)} %param.16) | copy-start | bytes 1540
  25.3 65.1 %copy-start.4 = (f32[2,256]{1,0:T(2,128)S(1)}, f32[2,256]{1,0:T(2,128)}, u32[]{:S(2)}) copy-start(f32[2,256]{1,0:T(2,128)} %param.13) | copy-start | bytes 6148
  25.3 65.2 %copy-start.5 = (f32[2,48]{1,0:T(2,128)S(1)}, f32[2,48]{1,0:T(2,128)}, u32[]{:S(2)}) copy-start(f32[2,48]{1,0:T(2,128)} %param.12) | copy-start | bytes 1156
  112.2 4.3 %copy-start.3 = (f32[3,1024]{1,0:T(4,128)S(1)}, f32[3,1024]{1,0:T(4,128)}, u32[]{:S(2)}) copy-start(f32[3,1024]{1,0:T(4,128)} %param.17) | copy-start | bytes 36868
  128.7 0.9 copy-start.1
  144.1 24.5 %copy-start.2 = (f32[2,8,3072]{2,1,0:T(8,128)}, f32[2,8,3072]{2,1,0:T(8,128)S(1)}, u32[]{:S(2)}) copy-start(f32[2,8,3072]{2,1,0:T(8,128)S(1)} %fusion.22) | copy-start | bytes 589828
Sparse Core Ops, SparseCore 0:
  90.2 22.4 reduce-scatter.1
where the time goes:
time: 176 us; the launch traced here: 175 us
  matrix products  71 us (40%)
  blocking collectives  55.3 us (31%)
  local copies, waits for them, and re-layouts  25.3 us (14%)
  between operations  14.3 us (8%)
  other arithmetic  9.37 us (5%)
    dot_general x1, matrix products, local(): jnp.einsum('csq,cqo->cso', fitted_low, factors, preferred_element_type=jn...  64.8 us
    gather x2, local copies, waits for them, and re-layouts, local(): gap = jnp.take(eps_vir, vir_of, axis=1) - jnp.take(eps_occ, occ_of, axis=1)  21.6 us
    all_gather x1, blocking collectives, local(): lax.all_gather(masked, 'inner', axis=2, tiled=True)  16.3 us
    psum x1, blocking collectives, local(): lax.psum((jnp.sum(current * image, axis=2), jnp.sum(current * current, ax...  12.4 us
    all_gather x1, blocking collectives, local(): lax.all_gather(slice_xyz, 'grp', axis=0, tiled=True)  9.24 us
    all_gather x1, blocking collectives, local(): lax.all_gather(slice_charges, 'grp', axis=0, tiled=True)  8.9 us
    psum x1, blocking collectives, local(): group_charges = lax.psum(partial_charges, 'inner')  8.5 us
    dot_general x2, matrix products, coupling_block(): jnp.einsum('csa,carb,rb->csr', group_charges, kernel, in_charges, precisi...  5.94 us
  transfers between devices with their start and end apart: 1, of which 0 were waited for; matrix products, arithmetic and copies ran while one was open for 17% of the time, Pallas kernels for 0%

commit v1 on v0

--- a/solution.py
+++ b/solution.py
@@ -6,6 +6,18 @@
 NVIR = 256
 STATES = 8
 epsilon = 1e-06
+
+
+def product_in_turn(shard, axis, dim, term):
+    size, place = (lax.axis_size(axis), lax.axis_index(axis))
+    left = [(i, (i - 1) % size) for i in range(size)]
+    extent = shard.shape[dim]
+    current = shard
+    total = term(current, place * extent)
+    for step in range(1, size):
+        current = lax.ppermute(current, axis, left)
+        total = total + term(current, (place + step) % size * extent)
+    return total
 
 
 def coupling_block(
@@ -43,11 +55,16 @@
     ).astype(jnp.float32)
     gap = jnp.take(eps_vir, vir_of, axis=1) - jnp.take(eps_occ, occ_of, axis=1)
     masked = amplitudes * active[:, None, :].astype(jnp.bfloat16)
-    fitted = jnp.einsum(
-        "cso,cqo->csq",
-        lax.all_gather(masked, "inner", axis=2, tiled=True),
-        factors,
-        preferred_element_type=jnp.float32,
+    fitted = product_in_turn(
+        masked,
+        "inner",
+        2,
+        lambda shard, start: jnp.einsum(
+            "cso,cqo->csq",
+            shard,
+            lax.dynamic_slice_in_dim(factors, start, shard.shape[2], axis=2),
+            preferred_element_type=jnp.float32,
+        ),
     )
     fitted_low = fitted.astype(jnp.bfloat16)
     current = masked.astype(jnp.float32)

time: 176 us -> 162 us (0.920)
  matrix products: 71 us -> 33 us
  local copies, waits for them, and re-layouts: 25.3 us -> 49.1 us
  blocking collectives: 55.3 us -> 37.3 us
  waiting for transfers between devices: 0.04 us -> 9.64 us
  starting transfers between devices: 0.04 us -> 7.63 us
    dot_general x1, matrix products: 64.8 us -> 13.4 us  [local(): jnp.einsum('csq,cqo->cso', fitted_low, factors, preferred_element_type=jn...]
    unnamed x18 -> x17, local copies, waits for them, and re-layouts: 1.06 us -> 24.7 us
    all_gather x1 -> x0, blocking collectives: 16.3 us -> none  [local(): lax.all_gather(masked, 'inner', axis=2, tiled=True)]
    dot_general x0 -> x3, matrix products: none -> 13.4 us  [local(): jnp.einsum('cso,cqo->csq', shard, lax.dynamic_slice_in_dim(factors, start...]
    reduce_scatter x1, waiting for transfers between devices: 0.02 us -> 9.61 us  [local(): lax.psum_scatter(partial_value, 'inner', scatter_dimension=2, tiled=True)]
    ppermute x0 -> x3, starting transfers between devices: none -> 7.59 us  [product_in_turn(): current = lax.ppermute(current, axis, left)]
    psum x1, blocking collectives: 12.4 us -> 8.52 us  [local(): lax.psum((jnp.sum(current * image, axis=2), jnp.sum(current * current, ax...]
    psum x1, blocking collectives: 8.5 us -> 10.3 us  [local(): group_charges = lax.psum(partial_charges, 'inner')]
  transfers between devices with their start and end apart: 1 -> 4, of which waited for: 0 -> 1; matrix products, arithmetic and copies ran while one was open for 17% -> 42% of each run, Pallas kernels for 0% -> 0%
where the time goes in v1:
time: 162 us; the launch traced here: 161 us
  local copies, waits for them, and re-layouts  49.1 us (30%)
  blocking collectives  37.3 us (23%)
  matrix products  33 us (20%)
  between operations  14.2 us (9%)
  other arithmetic  10.7 us (7%)
  waiting for transfers between devices  9.64 us (6%)
  starting transfers between devices  7.63 us (5%)
    unnamed x17, local copies, waits for them, and re-layouts  24.7 us
    gather x2, local copies, waits for them, and re-layouts, local(): gap = jnp.take(eps_vir, vir_of, axis=1) - jnp.take(eps_occ, occ_of, axis=1)  21.7 us
    dot_general x3, matrix products, local(): jnp.einsum('cso,cqo->csq', shard, lax.dynamic_slice_in_dim(factors, start...  13.4 us
    dot_general x1, matrix products, local(): jnp.einsum('csq,cqo->cso', fitted_low, factors, preferred_element_type=jn...  13.4 us
    psum x1, blocking collectives, local(): group_charges = lax.psum(partial_charges, 'inner')  10.3 us
    reduce_scatter x1, waiting for transfers between devices, local(): lax.psum_scatter(partial_value, 'inner', scatter_dimension=2, tiled=True)  9.61 us
    all_gather x1, blocking collectives, local(): lax.all_gather(slice_xyz, 'grp', axis=0, tiled=True)  9.39 us
    all_gather x1, blocking collectives, local(): lax.all_gather(slice_charges, 'grp', axis=0, tiled=True)  9.05 us
  transfers between devices with their start and end apart: 4, of which 1 were waited for; matrix products, arithmetic and copies ran while one was open for 42% of the time, Pallas kernels for 0%

profile of v1, /device:TPU:0, one launch (start us, length us, event | category | flops | bytes accessed | tf_op | source)
XLA Modules:
  0.0 161.5 jit_solution(7922822152425925926)
XLA Ops:
  7.3 0.8 fusion.49
  8.1 0.9 broadcast_multiply_fusion
  9.0 5.1 %collective-permute-start = (bf16[2,8,3072]{2,1,0:T(8,128)(2,1)S(1)}, bf16[2,8,3072]{2,1,0:T(8,128)(2,1)S(1)}, u32[]{:S(2)}, u32[]{:S(2)}) collective-permute-start(bf16[2,8,3072]{2,1,0:T(8,128)(2,1)S(1)} %broadcast_multiply_fusion), channel_id=1, source_target_pairs={{0,3},{1,0},{2,1},{3,2},{4,7},{5,4},{6,5},{7,6},{8,11},{9,8},{10,9... | collective-permute-start | bytes 294920 | tf_op jit(solution)/shard_map/ppermute | solution.py:18
  14.3 0.7 compare_select_fusion.9
  15.0 0.7 compare_and_fusion.3
  15.7 24.2 %copy.54 = bf16[2,500,12288]{2,1,0:T(8,128)(2,1)} copy(bf16[2,500,12288]{2,0,1:T(2,128)(2,1)} %param.10) | data formatting | bytes 49152000 | tf_op args[1]
  40.1 10.8 %gather_fusion = f32[3072,2]{1,0:T(8,128)} fusion(f32[2,256]{0,1:T(8,128)S(1)} %copy.51, s32[3072]{0:T(1024)S(1)} %broadcast_clamp_fusion.1), kind=kCustom, calls=%fused_computation | custom fusion | bytes 61440 | tf_op jit(solution)/shard_map/jit(_take)/gather | solution.py:56
  51.0 10.8 %gather_fusion.1 = f32[3072,2]{1,0:T(8,128)} fusion(f32[2,48]{0,1:T(8,128)S(1)} %copy.52, s32[3072]{0:T(1024)S(1)} %broadcast_clamp_fusion), kind=kCustom, calls=%fused_computation.1 | custom fusion | bytes 61440 | tf_op jit(solution)/shard_map/jit(_take)/gather | solution.py:56
  61.8 3.7 %subtract_bitcast_fusion = f32[2,3072]{0,1:T(8,128)S(1)} fusion(f32[3072,2]{1,0:T(8,128)} %gather_fusion.1, f32[3072,2]{1,0:T(8,128)} %gather_fusion, pred[3072]{0:T(1024)(128)(4,1)S(1)} %get-tuple-element.14, pred[3072]{0:T(1024)(128)(4,1)S(1)} %get-tuple-element.15), kind=kLoop, calls=%fused_computation.18 | loop fusion | flops 18432 | bytes 79872 | tf_op jit(solution)/shard_map/sub | solution.py:56
  67.1 4.5 %fusion.7 = f32[2,8,500]{2,1,0:T(8,128)S(1)} fusion(bf16[2,8,3072]{2,1,0:T(8,128)(2,1)S(1)} %broadcast_multiply_fusion, bf16[2,500,12288]{2,1,0:T(8,128)(2,1)} %copy.54, s32[]{:T(128)S(6)} %select_n.217), kind=kOutput, calls=%fused_computation.13 | convolution fusion | flops 49152000 | bytes 6323460 | tf_op jit(solution)/shard_map/cso,cqo->csq/dot_general | solution.py:62
  72.8 4.5 %fusion.11 = f32[2,8,500]{2,1,0:T(8,128)S(1)} fusion(f32[2,8,500]{2,1,0:T(8,128)S(1)} %fusion.7, bf16[2,8,3072]{2,1,0:T(8,128)(2,1)S(1)} %collective-permute-done, bf16[2,500,12288]{2,1,0:T(8,128)(2,1)} %copy.54, s32[]{:T(128)S(6)} %select_n.219), kind=kOutput, calls=%fused_computation.19 | convolution fusion | flops 49160000 | bytes 6355460 | tf_op jit(solution)/shard_map/cso,cqo->csq/dot_general | solution.py:62
  77.2 2.0 %collective-permute-start.2 = (bf16[2,8,3072]{2,1,0:T(8,128)(2,1)S(1)}, bf16[2,8,3072]{2,1,0:T(8,128)(2,1)S(1)}, u32[]{:S(2)}, u32[]{:S(2)}) collective-permute-start(bf16[2,8,3072]{2,1,0:T(8,128)(2,1)S(1)} %collective-permute-done.1), channel_id=1, source_target_pairs={{0,3},{1,0},{2,1},{3,2},{4,7},{5,4},{6,5},{7,6},{8,11},{9,8},{10,9... | collective-permute-start | bytes 294920 | tf_op jit(solution)/shard_map/ppermute | solution.py:18
  79.2 4.5 %fusion.14 = f32[2,8,500]{2,1,0:T(8,128)S(1)} fusion(f32[2,8,500]{2,1,0:T(8,128)S(1)} %fusion.11, bf16[2,8,3072]{2,1,0:T(8,128)(2,1)S(1)} %collective-permute-done.1, bf16[2,500,12288]{2,1,0:T(8,128)(2,1)} %copy.54, s32[]{:T(128)S(6)} %select_n.221), kind=kOutput, calls=%fused_computation.20 | convolution fusion | flops 49160000 | bytes 6355460 | tf_op jit(solution)/shard_map/cso,cqo->csq/dot_general | solution.py:62
  83.7 13.4 %fusion = bf16[2,8,12288]{2,1,0:T(8,128)(2,1)} fusion(bf16[2,500,12288]{2,1,0:T(8,128)(2,1)} %copy.54, f32[2,8,500]{2,1,0:T(8,128)S(1)} %fusion.14, bf16[2,8,3072]{2,1,0:T(8,128)(2,1)S(1)} %collective-permute-done.2, s32[]{:T(128)S(6)} %select_n.223), kind=kOutput, calls=%fused_computation.5 | convolution fusion | flops 246169216 | bytes 31489284 | tf_op jit(solution)/shard_map/csq,cqo->cso/dot_general | solution.py:72
  97.0 9.4 %all_gather.6 = f32[32,3,64]{2,1,0:T(4,128)S(1)} all-gather(f32[4,3,64]{2,1,0:T(4,128)S(1)} %broadcast_select_fusion), channel_id=1, replica_groups=mesh['grp'=8,'inner'=4] {'grp'}, dimensions={0}, use_global_device_ids=true | all-gather | bytes 27648 | tf_op jit(solution)/shard_map/all_gather | solution.py:107
  106.5 1.1 multiply_reduce_fusion
  107.9 9.6 %reduce-scatter.2.cloned.1.call-done = bf16[2,8,3072]{2,1,0:T(8,128)(2,1)} async-done(((bf16[2,8,12288]{2,1,0:T(8,128)(2,1)}), bf16[2,8,3072]{2,1,0:T(8,128)(2,1)}) %reduce-scatter.2.cloned.1.call-update) | async-done | bytes 98320 | tf_op jit(solution)/shard_map/reduce_scatter | solution.py:74
  117.5 1.1 fusion.27
  118.6 8.5 %all-reduce = (f32[2,8]{1,0:T(2,128)S(1)}, f32[2,8]{1,0:T(2,128)S(1)}) all-reduce(f32[2,8]{1,0:T(2,128)S(1)} %get-tuple-element.5, f32[2,8]{1,0:T(2,128)S(1)} %get-tuple-element.4), channel_id=1, replica_groups=mesh['grp'=8,'inner'=4] {'inner'}, use_global_device_ids=true, to_apply=%region_2.3 | all-reduce | flops 32 | bytes 256 | tf_op jit(solution)/shard_map/psum | solution.py:78
  127.1 1.0 fusion.30
  128.5 10.3 %psum.23 = f32[16,64]{1,0:T(8,128)S(1)} all-reduce(f32[16,64]{1,0:T(8,128)S(1)} %convolution_bitcast_fusion), channel_id=1, replica_groups=mesh['grp'=8,'inner'=4] {'inner'}, use_global_device_ids=true, to_apply=%region_5.6 | all-reduce | flops 1024 | bytes 8192 | tf_op jit(solution)/shard_map/psum | solution.py:90
  138.8 9.1 %all-gather = f32[8,4,64]{2,1,0:T(4,128)S(1)} all-gather(f32[1,4,64]{2,1,0:T(4,128)S(1)} %dynamic-slice_bitcast_fusion), channel_id=1, replica_groups=mesh['grp'=8,'inner'=4] {'grp'}, dimensions={0}, use_global_device_ids=true | all-gather | bytes 9216 | tf_op jit(solution)/shard_map/all_gather | solution.py:106
  147.9 5.8 %fusion.9 = f32[32,1,2,64]{3,1,2,0:T(1,128)S(1)} fusion(f32[32,64,1,1]{1,2,3,0:T(1,128)S(1)} %bitcast.38, f32[2,64,32,64]{3,2,1,0:T(8,128)S(1)} %add_rsqrt_fusion), kind=kOutput, calls=%fused_computation.15 | convolution fusion | flops 3145728 | bytes 1073152 | tf_op jit(solution)/shard_map/csa,carb,rb->csr/dot_general | solution.py:29
  153.9 0.7 reshape_reshape.3
  (48 shorter events, 4.2 us)
Async XLA Ops:
  7.2 121.0 %copy-start = (bf16[2,64,3072]{2,1,0:T(8,128)(2,1)S(1)}, bf16[2,64,3072]{2,1,0:T(8,128)(2,1)}, u32[]{:S(2)}) copy-start(bf16[2,64,3072]{2,1,0:T(8,128)(2,1)} %param.11) | copy-start | bytes 2359300
  7.2 110.4 %reduce-scatter.2.cloned.1.call-start = ((), (), s32[]{:S(2)}) async-start(), calls=%async_computation.1 | async-start | bytes 491520 | tf_op jit(solution)/shard_map/reduce_scatter | solution.py:74
  9.0 63.3 %collective-permute-start = (bf16[2,8,3072]{2,1,0:T(8,128)(2,1)S(1)}, bf16[2,8,3072]{2,1,0:T(8,128)(2,1)S(1)}, u32[]{:S(2)}, u32[]{:S(2)}) collective-permute-start(bf16[2,8,3072]{2,1,0:T(8,128)(2,1)S(1)} %broadcast_multiply_fusion), channel_id=1, source_target_pairs={{0,3},{1,0},{2,1},{3,2},{4,7},{5,4},{6,5},{7,6},{8,11},{9,8},{10,9... | collective-permute-start | bytes 294920 | tf_op jit(solution)/shard_map/ppermute | solution.py:18
  15.7 24.2 %copy-start.4 = (f32[2,256]{1,0:T(2,128)S(1)}, f32[2,256]{1,0:T(2,128)}, u32[]{:S(2)}) copy-start(f32[2,256]{1,0:T(2,128)} %param.13) | copy-start | bytes 6148
  15.7 24.4 %copy-start.5 = (f32[2,48]{1,0:T(2,128)S(1)}, f32[2,48]{1,0:T(2,128)}, u32[]{:S(2)}) copy-start(f32[2,48]{1,0:T(2,128)} %param.12) | copy-start | bytes 1156
  39.9 26.2 %copy-start.3 = (f32[3,1024]{1,0:T(4,128)S(1)}, f32[3,1024]{1,0:T(4,128)}, u32[]{:S(2)}) copy-start(f32[3,1024]{1,0:T(4,128)} %param.17) | copy-start | bytes 36868
  72.3 5.0 %collective-permute-start.1 = (bf16[2,8,3072]{2,1,0:T(8,128)(2,1)S(1)}, bf16[2,8,3072]{2,1,0:T(8,128)(2,1)S(1)}, u32[]{:S(2)}, u32[]{:S(2)}) collective-permute-start(bf16[2,8,3072]{2,1,0:T(8,128)(2,1)S(1)} %collective-permute-done), channel_id=1, source_target_pairs={{0,3},{1,0},{2,1},{3,2},{4,7},{5,4},{6,5},{7,6},{8,11},{9,8},{10,9... | collective-permute-start | bytes 294920 | tf_op jit(solution)/shard_map/ppermute | solution.py:18
  77.2 6.4 %collective-permute-start.2 = (bf16[2,8,3072]{2,1,0:T(8,128)(2,1)S(1)}, bf16[2,8,3072]{2,1,0:T(8,128)(2,1)S(1)}, u32[]{:S(2)}, u32[]{:S(2)}) collective-permute-start(bf16[2,8,3072]{2,1,0:T(8,128)(2,1)S(1)} %collective-permute-done.1), channel_id=1, source_target_pairs={{0,3},{1,0},{2,1},{3,2},{4,7},{5,4},{6,5},{7,6},{8,11},{9,8},{10,9... | collective-permute-start | bytes 294920 | tf_op jit(solution)/shard_map/ppermute | solution.py:18
  97.0 20.5 %copy-start.1 = (bf16[2,8,3072]{2,1,0:T(8,128)(2,1)S(1)}, bf16[2,8,3072]{2,1,0:T(8,128)(2,1)}, u32[]{:S(2)}) copy-start(bf16[2,8,3072]{2,1,0:T(8,128)(2,1)} %param.9) | copy-start | bytes 294916
  128.1 26.5 %copy-start.2 = (f32[2,8,3072]{2,1,0:T(8,128)}, f32[2,8,3072]{2,1,0:T(8,128)S(1)}, u32[]{:S(2)}) copy-start(f32[2,8,3072]{2,1,0:T(8,128)S(1)} %fusion.30) | copy-start | bytes 589828
Sparse Core Ops, SparseCore 0:
  97.2 20.3 reduce-scatter.1
